TPU v7x, 1024 devices: a whole 8x8x8 slice. The times are simulated.
1024 devices in a mesh: seq: 16 (over y, core), tp: 8 (over z), dp: 8 (over x).
Axes of the slice: x: 8, y: 8, z: 8, core: 2. Of those that a mesh axis runs over, the one named last changes fastest.
Arguments:
- queries: bfloat16 [32768, 4096], P(('dp', 'seq'), 'tp'), parts along dimension 0, may hold values from -36 to 36
- key_rows: bfloat16 [32768, 4096], P(('dp', 'seq'), 'tp'), parts along dimension 0, may hold values from -36 to 36
- values: bfloat16 [32768, 4096], P(('dp', 'seq'), 'tp'), parts along dimension 0, may hold values from -6 to 6
- modality: int32 [32768], P(('dp', 'seq')), parts along dimension 0, may hold values from 0 to 1, as said below
- out_weight: bfloat16 [2, 4096, 4096], P(None, 'tp'), may hold values from -0.125 to 0.125
Outputs:
- layer_out: bfloat16 [32768, 4096], P(('dp', 'seq'), 'tp'), parts along dimension 0
There are 8 independent parts, one for each index of `dp`. A program takes and returns all parts, laid end to end along the dimension named above; an argument that names none is the same for every part. Nothing has to cross between parts.
Inputs may be any that keep to these rules, and one draw needn't show every extreme that they name: `modality`: 1 marks an image token, 0 a text token.
All inputs are finite; a program needn't handle non-finite values.
Results may differ from a plain program's by a relative error of at most 0.013.
Values may be sent and summed in bfloat16 or wider, within the bound.
A program may use at most 64 MiB of HBM per device.

v0:
```python
import math

import jax
import jax.numpy as jnp
from jax import lax
from jax.sharding import PartitionSpec as P

HD = 128


def cut_along(x, dim, size):
    shape = x.shape
    blocks = x.reshape(*shape[:dim], size, shape[dim] // size, *shape[dim + 1 :])
    return jnp.moveaxis(blocks, dim, 0)


def sum_at_owner(x, axis, dim):
    blocks = cut_along(x, dim, lax.axis_size(axis))
    arrived = lax.all_to_all(blocks, axis, split_axis=0, concat_axis=0, tiled=True)
    return arrived.astype(jnp.float32).sum(axis=0)


def attend(parts, my_group, sub_rows, token_rows):
    query_part, key_part, value_part = parts
    queries_all = query_part[0]
    keys_all = key_part[0]
    values_all = value_part[0]
    length = queries_all.shape[0]
    heads_now = queries_all.shape[1]
    head_width = queries_all.shape[2]
    block_rows = math.gcd(length, 512)
    blocks = length // block_rows
    score_scale = head_width ** (-0.5)
    local_rows = jnp.arange(length, dtype=jnp.int32)
    positions = local_rows // sub_rows * token_rows + my_group * sub_rows + local_rows % sub_rows
    key_positions = jnp.arange(keys_all.shape[0], dtype=jnp.int32)

    def one_block(inputs):
        query_block, position_block = inputs
        scores = (
            jnp.einsum("qhd,khd->hqk", query_block, keys_all, preferred_element_type=jnp.float32)
            * score_scale
        )
        allowed = position_block[:, None] >= key_positions[None, :]
        scores = jnp.where(allowed[None], scores, -jnp.inf)
        largest = jnp.max(scores, axis=2, keepdims=True)
        weights = jnp.exp(scores - largest)
        probabilities = (weights / jnp.sum(weights, axis=2, keepdims=True)).astype(jnp.bfloat16)
        return jnp.einsum(
            "hqk,khd->qhd", probabilities, values_all, preferred_element_type=jnp.float32
        ).astype(jnp.bfloat16)

    result = lax.map(
        one_block,
        (
            queries_all.reshape(blocks, block_rows, heads_now, head_width),
            positions.reshape(blocks, block_rows),
        ),
    )
    return result.reshape(1, length, heads_now, head_width)


def on_device(queries, key_rows, values, modality, out_weight):
    seq_count = lax.axis_size("seq")
    token_rows = queries.shape[0]
    head_width = HD
    heads_here = queries.shape[1] // head_width
    per_device = max(1, heads_here // seq_count)
    groups = max(1, seq_count // heads_here)
    head_sets = heads_here // per_device
    sub_rows = token_rows // groups
    my_group = lax.axis_index("seq") % groups
    query_items = queries.reshape(groups, sub_rows, head_sets, per_device, head_width)
    query_items = query_items.transpose(2, 0, 1, 3, 4).reshape(
        seq_count, sub_rows, per_device, head_width
    )

    def spread(field):
        shaped = field.reshape(token_rows, head_sets, per_device, head_width).transpose(1, 0, 2, 3)
        widened = jnp.broadcast_to(
            shaped[:, None], (head_sets, groups, token_rows, per_device, head_width)
        )
        return widened.reshape(seq_count, token_rows, per_device, head_width)

    exchanged = attend(
        (
            lax.all_to_all(query_items, "seq", split_axis=0, concat_axis=1, tiled=True),
            lax.all_to_all(spread(key_rows), "seq", split_axis=0, concat_axis=1, tiled=True),
            lax.all_to_all(spread(values), "seq", split_axis=0, concat_axis=1, tiled=True),
        ),
        my_group,
        sub_rows,
        token_rows,
    )
    returned = lax.all_to_all(
        exchanged.reshape(seq_count, sub_rows, per_device, head_width),
        "seq",
        split_axis=0,
        concat_axis=0,
        tiled=True,
    )
    attended = returned.reshape(head_sets, groups, sub_rows, per_device, head_width)
    attended = attended.transpose(1, 2, 0, 3, 4).reshape(token_rows, heads_here * head_width)
    tile_rows = math.gcd(token_rows, 128)
    tile_count = token_rows // tile_rows

    def project(inputs):
        rows_in, token_kinds = inputs
        first_kind = token_kinds[0]

        def single(tile_block):
            return jnp.dot(tile_block, out_weight[first_kind], preferred_element_type=jnp.float32)

        def both_kinds(tile_block):
            text_part = jnp.dot(tile_block, out_weight[0], preferred_element_type=jnp.float32)
            image_part = jnp.dot(tile_block, out_weight[1], preferred_element_type=jnp.float32)
            return jnp.where(token_kinds[:, None] == 1, image_part, text_part)

        return lax.cond(jnp.all(token_kinds == first_kind), single, both_kinds, rows_in)

    partial_value = lax.map(
        project,
        (
            attended.reshape(tile_count, tile_rows, heads_here * head_width),
            modality.reshape(tile_count, tile_rows),
        ),
    )
    partial_value = partial_value.reshape(token_rows, out_weight.shape[2])
    return sum_at_owner(partial_value.astype(jnp.bfloat16), "tp", 1).astype(jnp.bfloat16)


def solution(mesh):
    in_specs = (
        P(("dp", "seq"), "tp"),
        P(("dp", "seq"), "tp"),
        P(("dp", "seq"), "tp"),
        P(("dp", "seq")),
        P(None, "tp", None),
    )
    out_specs = P(("dp", "seq"), "tp")
    return jax.shard_map(
        on_device, mesh=mesh, in_specs=in_specs, out_specs=out_specs, check_vma=False
    )
```

profile of v0, /device:TPU:1, one launch (start us, length us, event | category | flops | bytes accessed | tf_op | source)
XLA Modules:
  0.0 200.1 jit_solution(17614110026527079401)
XLA Ops:
  0.0 1.0 reshape.96
  1.0 0.8 copy.24
  1.8 17.4 %all-to-all-start = ((bf16[16,64,1,128]{3,1,2,0:T(8,128)(2,1)}), bf16[16,64,1,128]{3,1,2,0:T(8,128)(2,1)S(1)}, u32[]{:S(2)}, u32[]{:S(2)}) async-start(bf16[16,64,1,128]{3,1,2,0:T(8,128)(2,1)} %bitcast.11), calls=%async_computation | async-start | bytes 524288 | tf_op jit(solution)/shard_map/all_to_all | solution.py:87
  19.2 1.0 reshape.98
  20.3 10.7 %all-to-all-done = bf16[16,64,1,128]{3,1,2,0:T(8,128)(2,1)S(1)} async-done(((bf16[16,64,1,128]{3,1,2,0:T(8,128)(2,1)}), bf16[16,64,1,128]{3,1,2,0:T(8,128)(2,1)S(1)}, u32[]{:S(2)}, u32[]{:S(2)}) %all-to-all-start) | async-done | bytes 262176 | tf_op jit(solution)/shard_map/all_to_all | solution.py:87
  31.0 1.2 broadcast_in_dim.59
  32.1 3.5 %all-to-all-start.1 = ((bf16[16,256,1,128]{3,1,2,0:T(8,128)(2,1)}), bf16[16,256,1,128]{3,1,2,0:T(8,128)(2,1)S(1)}, u32[]{:S(2)}, u32[]{:S(2)}) async-start(bf16[16,256,1,128]{3,1,2,0:T(8,128)(2,1)} %bitcast.16), calls=%async_computation.1 | async-start | bytes 2097152 | tf_op jit(solution)/shard_map/all_to_all | solution.py:88
  35.7 1.0 reshape.99
  36.8 26.0 %all-to-all-done.1 = bf16[16,256,1,128]{3,1,2,0:T(8,128)(2,1)S(1)} async-done(((bf16[16,256,1,128]{3,1,2,0:T(8,128)(2,1)}), bf16[16,256,1,128]{3,1,2,0:T(8,128)(2,1)S(1)}, u32[]{:S(2)}, u32[]{:S(2)}) %all-to-all-start.1) | async-done | bytes 1048608 | tf_op jit(solution)/shard_map/all_to_all | solution.py:88
  62.7 1.2 broadcast_in_dim.62
  63.9 3.7 %all-to-all-start.2 = ((bf16[16,256,1,128]{3,1,2,0:T(8,128)(2,1)}), bf16[16,256,1,128]{3,1,2,0:T(8,128)(2,1)S(1)}, u32[]{:S(2)}, u32[]{:S(2)}) async-start(bf16[16,256,1,128]{3,1,2,0:T(8,128)(2,1)} %bitcast.20), calls=%async_computation.2 | async-start | bytes 2097152 | tf_op jit(solution)/shard_map/all_to_all | solution.py:89
  67.7 27.9 %all-to-all-done.2 = bf16[16,256,1,128]{3,1,2,0:T(8,128)(2,1)S(1)} async-done(((bf16[16,256,1,128]{3,1,2,0:T(8,128)(2,1)}), bf16[16,256,1,128]{3,1,2,0:T(8,128)(2,1)S(1)}, u32[]{:S(2)}, u32[]{:S(2)}) %all-to-all-start.2) | async-done | bytes 1048608 | tf_op jit(solution)/shard_map/all_to_all | solution.py:89
  95.6 12.1 %while.22 = (s32[]{:T(128)}, bf16[2,512,1,128]{3,1,2,0:T(8,128)(2,1)}, s32[2,512]{1,0:T(2,128)S(1)}, bf16[2,512,1,128]{3,1,2,0:T(8,128)(2,1)S(1)}, bf16[4096,1,1...) while((s32[]{:T(128)}, bf16[2,512,1,128]{3,1,2,0:T(8,128)(2,1)}, ...), condition=%wide.region_3.4_spmd.clone, body=%wide.region_0.3_spmd.clone.sunk | while | flops 1092680704 | bytes 27542100 | solution.py:53
  95.7 1.9 fusion.34
  97.6 1.3 fusion.35
  98.9 2.8 %fusion.36 = bf16[2,512,1,128]{3,1,2,0:T(8,128)(2,1)} fusion(bf16[2,512,1,128]{3,1,2,0:T(8,128)(2,1)} %get-tuple-element.229, s32[]{:T(128)} %get-tuple-element.228, f32[512,4096]{1,0:T(8,128)S(1)} %get-tuple-element.219, f32[512]{0:T(512)S(1)} %fusion.35, f32[512]{0:T(512)S(1)} %get-tuple-element.220, bf16[4096,1,128]{2,0,1:T(8,128)(2,1)S(1)} %get-tuple-element.240), kind=kOutput, calls=%fused_computation.25.clone.1 | convolution fusion | flops 543227904 | bytes 9572864 | tf_op jit(solution)/shard_map/while/body/eval_jaxpr/hqk,khd->qhd/dot_general | solution.py:49
  101.7 1.9 fusion.34
  103.6 1.3 fusion.35
  104.9 2.8 %fusion.36 = bf16[2,512,1,128]{3,1,2,0:T(8,128)(2,1)} fusion(bf16[2,512,1,128]{3,1,2,0:T(8,128)(2,1)} %get-tuple-element.229, s32[]{:T(128)} %get-tuple-element.228, f32[512,4096]{1,0:T(8,128)S(1)} %get-tuple-element.219, f32[512]{0:T(512)S(1)} %fusion.35, f32[512]{0:T(512)S(1)} %get-tuple-element.220, bf16[4096,1,128]{2,0,1:T(8,128)(2,1)S(1)} %get-tuple-element.240), kind=kOutput, calls=%fused_computation.25.clone.1 | convolution fusion | flops 543227904 | bytes 9572864 | tf_op jit(solution)/shard_map/while/body/eval_jaxpr/hqk,khd->qhd/dot_general | solution.py:49
  107.7 3.4 %all-to-all-start.3 = ((bf16[16,64,1,128]{3,1,2,0:T(8,128)(2,1)}), bf16[16,64,1,128]{3,1,2,0:T(8,128)(2,1)S(1)}, u32[]{:S(2)}, u32[]{:S(2)}) async-start(bf16[16,64,1,128]{3,1,2,0:T(8,128)(2,1)} %bitcast.22), calls=%async_computation.3 | async-start | bytes 524288 | tf_op jit(solution)/shard_map/all_to_all | solution.py:95
  111.2 11.6 %all-to-all-done.3 = bf16[16,64,1,128]{3,1,2,0:T(8,128)(2,1)S(1)} async-done(((bf16[16,64,1,128]{3,1,2,0:T(8,128)(2,1)}), bf16[16,64,1,128]{3,1,2,0:T(8,128)(2,1)S(1)}, u32[]{:S(2)}, u32[]{:S(2)}) %all-to-all-start.3) | async-done | bytes 262176 | tf_op jit(solution)/shard_map/all_to_all | solution.py:95
  123.1 13.2 %while.21 = (s32[]{:T(128)}, bf16[2,128,4096]{2,1,0:T(8,128)(2,1)}, s32[2,128]{1,0:T(2,128)S(1)}, bf16[2,128,512]{2,1,0:T(8,128)(2,1)S(1)}, bf16[2,512,4096]{2,1,0:T(8,128)(2,1)}, /*index=5*/s32[]{:T(128)}) while((s32[]{:T(128)}, bf16[2,128,4096]{2,1,0:T(8,128)(2,1)}, s32[2,128]{1,0:T(2,128)S(1)}, bf16[2,128,512]{2,1,0:T(8,128)(2,1)S(1)}, ...), condition=%wide.region_8.9_spmd, body=%wide.region_4.8_spmd.sunk | while | flops 1074266496 | bytes 14159767 | solution.py:121
  124.5 4.2 %conditional.2 = (bf16[1,128,4096]{2,1,0:T(8,128)(2,1)S(1)}) conditional(s32[]{:T(128)} %convert_element_type.51, (s32[128]{0:T(128)S(1)}, bf16[2,512,4096]{2,1,0:T(8,128)(2,1)}, bf16[128,512]{1,0:T(8,128)(2,1)S(1)}) %tuple.48, (s32[]{:T(128)S(1)}, bf16[2,512,4096]{2,1,0:T(8,128)(2,1)}, bf16[128,512]{1,0:T(8,128)(2,1)S(1)}) %tuple.63), branch_computations={%region_6.6_spmd, %region_7.7_spmd} | conditional | flops 1074266240 | bytes 11797256 | solution.py:119
  124.6 3.5 %convolution_bitcast_fusion = bf16[1,128,4096]{1,2,0:T(8,128)(2,1)S(1)} fusion(bf16[128,512]{1,0:T(8,128)(2,1)S(1)} %get-tuple-element.82, bf16[2,512,4096]{2,1,0:T(8,128)(2,1)} %get-tuple-element.80, s32[]{:T(128)S(6)} %select_n.28), kind=kOutput, calls=%fused_computation.9 | convolution fusion | flops 536870912 | bytes 5373956 | tf_op jit(solution)/shard_map/while/body/eval_jaxpr/cond/branch_1_fun/dot_general | solution.py:112
  128.6 1.0 constant_dynamic-update-slice_fusion.2
  129.7 0.7 compare_reduce_fusion.2
  131.0 4.2 %conditional.2 = (bf16[1,128,4096]{2,1,0:T(8,128)(2,1)S(1)}) conditional(s32[]{:T(128)} %convert_element_type.51, (s32[128]{0:T(128)S(1)}, bf16[2,512,4096]{2,1,0:T(8,128)(2,1)}, bf16[128,512]{1,0:T(8,128)(2,1)S(1)}) %tuple.48, (s32[]{:T(128)S(1)}, bf16[2,512,4096]{2,1,0:T(8,128)(2,1)}, bf16[128,512]{1,0:T(8,128)(2,1)S(1)}) %tuple.63), branch_computations={%region_6.6_spmd, %region_7.7_spmd} | conditional | flops 1074266240 | bytes 11797256 | solution.py:119
  131.2 3.5 %convolution_bitcast_fusion = bf16[1,128,4096]{1,2,0:T(8,128)(2,1)S(1)} fusion(bf16[128,512]{1,0:T(8,128)(2,1)S(1)} %get-tuple-element.82, bf16[2,512,4096]{2,1,0:T(8,128)(2,1)} %get-tuple-element.80, s32[]{:T(128)S(6)} %select_n.28), kind=kOutput, calls=%fused_computation.9 | convolution fusion | flops 536870912 | bytes 5373956 | tf_op jit(solution)/shard_map/while/body/eval_jaxpr/cond/branch_1_fun/dot_general | solution.py:112
  135.2 1.1 constant_dynamic-update-slice_fusion.2
  136.3 2.5 %copy.30 = bf16[32,8,8,512]{3,2,1,0:T(8,128)(2,1)S(1)} copy(bf16[32,8,8,512]{3,1,2,0:T(8,128)(2,1)} %bitcast.98) | data formatting | bytes 4194304
  139.5 59.6 %all_to_all.37 = bf16[8,256,512]{2,1,0:T(8,128)(2,1)S(1)} all-to-all(bf16[8,256,512]{2,1,0:T(8,128)(2,1)S(1)} %copy.29), channel_id=1, replica_groups=mesh['seq'=16,'tp'=8,'dp'=8] {'tp'}, dimensions={0} | all-to-all | bytes 4194304 | tf_op jit(solution)/shard_map/all_to_all | solution.py:19
  199.1 1.0 reduce_sum.21
  (21 shorter events, 2.9 us)
Async XLA Ops:
  1.8 29.2 %all-to-all-start = ((bf16[16,64,1,128]{3,1,2,0:T(8,128)(2,1)}), bf16[16,64,1,128]{3,1,2,0:T(8,128)(2,1)S(1)}, u32[]{:S(2)}, u32[]{:S(2)}) async-start(bf16[16,64,1,128]{3,1,2,0:T(8,128)(2,1)} %bitcast.11), calls=%async_computation | async-start | bytes 524288 | tf_op jit(solution)/shard_map/all_to_all | solution.py:87
  32.1 30.6 %all-to-all-start.1 = ((bf16[16,256,1,128]{3,1,2,0:T(8,128)(2,1)}), bf16[16,256,1,128]{3,1,2,0:T(8,128)(2,1)S(1)}, u32[]{:S(2)}, u32[]{:S(2)}) async-start(bf16[16,256,1,128]{3,1,2,0:T(8,128)(2,1)} %bitcast.16), calls=%async_computation.1 | async-start | bytes 2097152 | tf_op jit(solution)/shard_map/all_to_all | solution.py:88
  63.9 31.7 %all-to-all-start.2 = ((bf16[16,256,1,128]{3,1,2,0:T(8,128)(2,1)}), bf16[16,256,1,128]{3,1,2,0:T(8,128)(2,1)S(1)}, u32[]{:S(2)}, u32[]{:S(2)}) async-start(bf16[16,256,1,128]{3,1,2,0:T(8,128)(2,1)} %bitcast.20), calls=%async_computation.2 | async-start | bytes 2097152 | tf_op jit(solution)/shard_map/all_to_all | solution.py:89
  95.6 27.4 %copy-start = (s32[256]{0:T(256)S(1)}, s32[256]{0:T(256)}, u32[]{:S(2)}) copy-start(s32[256]{0:T(256)} %param.14) | copy-start | bytes 3076
  107.7 15.0 %all-to-all-start.3 = ((bf16[16,64,1,128]{3,1,2,0:T(8,128)(2,1)}), bf16[16,64,1,128]{3,1,2,0:T(8,128)(2,1)S(1)}, u32[]{:S(2)}, u32[]{:S(2)}) async-start(bf16[16,64,1,128]{3,1,2,0:T(8,128)(2,1)} %bitcast.22), calls=%async_computation.3 | async-start | bytes 524288 | tf_op jit(solution)/shard_map/all_to_all | solution.py:95
where the time goes:
time: 202 us; the launch traced here: 200 us
  waiting for transfers between devices  76.2 us (38%)
  blocking collectives  59.6 us (30%)
  starting transfers between devices  28.2 us (14%)
  matrix products  16.5 us (8%)
  local copies, waits for them, and re-layouts  13 us (6%)
  other arithmetic  4.98 us (2%)
    all_to_all x1, blocking collectives, sum_at_owner(): lax.all_to_all(blocks, axis, split_axis=0, concat_axis=0, tiled=True)  59.6 us
    all_to_all x1, waiting for transfers between devices, on_device(): lax.all_to_all(spread(values), 'seq', split_axis=0, concat_axis=1, tiled=...  27.9 us
    all_to_all x1, waiting for transfers between devices, on_device(): lax.all_to_all(spread(key_rows), 'seq', split_axis=0, concat_axis=1, tile...  26 us
    all_to_all x1, starting transfers between devices, on_device(): lax.all_to_all(query_items, 'seq', split_axis=0, concat_axis=1, tiled=True)  17.4 us
    all_to_all x1, waiting for transfers between devices, on_device(): lax.all_to_all(exchanged.reshape(seq_count, sub_rows, per_device, head_wi...  11.6 us
    all_to_all x1, waiting for transfers between devices, on_device(): lax.all_to_all(query_items, 'seq', split_axis=0, concat_axis=1, tiled=True)  10.7 us
    dot_general x2, matrix products, single(): jnp.dot(tile_block, out_weight[first_kind], preferred_element_type=jnp.fl...  7 us
    dot_general x2, matrix products, one_block(): jnp.einsum('hqk,khd->qhd', probabilities, values_all, preferred_element_t...  5.66 us
  transfers between devices with their start and end apart: 4, of which 4 were waited for; matrix products, arithmetic and copies ran while one was open for 1% of the time, Pallas kernels for 0%

commit v1 on v0

v1 whole, which is shorter than its diff:
```python
import functools

import jax
import jax.numpy as jnp
from jax import lax
from jax.experimental import pallas as pl
from jax.experimental.pallas import tpu as pltpu
from jax.sharding import PartitionSpec as P

HD = 128
N_TP = 8
MESH = pl.DeviceIdType.MESH
LOG2E = 1.4426950408889634


def fused(
    q_hbm, k_hbm, v_hbm, mod_ref, w_hbm, out_ref,
    qbuf, kbuf, vbuf, mbuf, acc, obuf, abuf, acat, wbuf, psum, rsnd, rrcv,
    local_sem, ksem, vsem, qsem, asem, rsem, q_send, kv_send, fwd_send, rel_send, o_send, r_send,
):
    me = lax.axis_index("seq")
    z = lax.axis_index("tp")
    rows = q_hbm.shape[0]
    half = rows // 2
    cols = out_ref.shape[1]
    y = me // 2
    c = me % 2
    side = y % 2
    out_dir = 2 * side - 1
    head = y // 2
    twin = 1 - 2 * c + me
    mate_chip = y - out_dir
    mate = mate_chip * 2 + c
    factor = HD ** (-0.5) * LOG2E

    def chip(t):
        return lax.rem(t + 16, 8)

    def send(src, dst, ssem, rsem_, seq):
        copy = pltpu.make_async_remote_copy(
            src_ref=src, dst_ref=dst, send_sem=ssem, recv_sem=rsem_,
            device_id={"seq": seq}, device_id_type=MESH,
        )
        return copy

    def k_at(slot):
        return kbuf.at[slot]

    def v_at(slot):
        return vbuf.at[slot, :, pl.ds(0, HD)]

    def head_cols(ref, h):
        return ref.at[:, pl.ds(pl.multiple_of(h * HD, HD), HD)]

    def await_kv(slot):
        send(k_at(slot), k_at(slot), local_sem.at[0], ksem.at[slot], twin).wait_recv()
        send(v_at(slot), v_at(slot), local_sem.at[0], vsem.at[slot], twin).wait_recv()

    own = [
        pltpu.make_async_copy(head_cols(k_hbm, head), k_at(me), ksem.at[me]),
        pltpu.make_async_copy(head_cols(v_hbm, head), v_at(me), vsem.at[me]),
        pltpu.make_async_copy(
            q_hbm.at[pl.ds(pl.multiple_of(c * half, half), half), pl.ds(pl.multiple_of(head * HD, HD), HD)],
            qbuf.at[0, pl.ds(pl.multiple_of(c * half, half), half), :],
            qsem.at[0, c],
        ),
    ]
    for copy in own:
        copy.start()
    w_copy = pltpu.make_async_copy(w_hbm, wbuf, local_sem.at[1])
    w_copy.start()

    barrier = pltpu.get_barrier_semaphore()
    left, right = lax.rem(z + N_TP - 1, N_TP), lax.rem(z + 1, N_TP)
    peers = 0
    for step in (1, 2, 3, -1, -2):
        for core in range(2):
            pl.semaphore_signal(
                barrier, inc=1, device_id={"seq": chip(y + out_dir * step) * 2 + core}, device_id_type=MESH
            )
            peers += 1
    pl.semaphore_signal(barrier, inc=1, device_id={"seq": twin}, device_id_type=MESH)
    for neighbour in (left, right):
        pl.semaphore_signal(barrier, inc=1, device_id={"tp": neighbour}, device_id_type=MESH)
    mbuf[...] = jnp.full(mbuf.shape, -jnp.inf, jnp.float32)
    acc[...] = jnp.zeros(acc.shape, jnp.float32)
    vbuf[:, :, HD:] = jnp.ones((vbuf.shape[0], rows, HD), jnp.bfloat16)
    pl.semaphore_wait(barrier, peers + 3)

    targets = {1: chip(y + out_dir), 3: chip(y + 3 * out_dir), 2: chip(y - 2 * out_dir)}
    pending = []

    def q_rows(core, h):
        return q_hbm.at[pl.ds(pl.multiple_of(core * half, half), half), pl.ds(pl.multiple_of(h * HD, HD), HD)]

    def q_slot(block):
        return qbuf.at[block, pl.ds(pl.multiple_of(c * half, half), half), :]

    pending.append(send(q_rows(1 - c, head), q_slot(0), q_send.at[0, 0], qsem.at[0, c], twin))
    pending.append(send(head_cols(k_hbm, head), k_at(me), rel_send.at[0, 0], ksem.at[me], twin))
    pending.append(send(head_cols(v_hbm, head), v_at(me), rel_send.at[0, 1], vsem.at[me], twin))
    for k in (3, 2, 1):
        chip_k = targets[k]
        for core in range(2):
            pending.append(
                send(q_rows(core, chip_k // 2), q_slot(k), q_send.at[k, core], qsem.at[k, c], chip_k * 2 + core)
            )
    for k in (2, 3, 1):
        chip_k = targets[k]
        pending.append(send(head_cols(k_hbm, chip_k // 2), k_at(me), kv_send.at[k, 0], ksem.at[me], chip_k * 2 + c))
        pending.append(send(head_cols(v_hbm, chip_k // 2), v_at(me), kv_send.at[k, 1], vsem.at[me], chip_k * 2 + c))
        if k == 2:
            pending.append(send(head_cols(k_hbm, head), k_at(me), kv_send.at[0, 0], ksem.at[me], mate))
            pending.append(send(head_cols(v_hbm, head), v_at(me), kv_send.at[0, 1], vsem.at[me], mate))
    for copy in pending:
        copy.start()

    def forwards(k):
        slot = chip(y + out_dir * k) * 2 + c
        return (
            send(k_at(slot), k_at(slot), fwd_send.at[k, 0], ksem.at[slot], mate),
            send(v_at(slot), v_at(slot), fwd_send.at[k, 1], vsem.at[slot], mate),
            send(k_at(slot), k_at(slot), fwd_send.at[k, 2], ksem.at[slot], twin),
            send(v_at(slot), v_at(slot), fwd_send.at[k, 3], vsem.at[slot], twin),
        )

    def relays(k):
        slot = chip(mate_chip - out_dir * k) * 2 + c
        return (
            send(k_at(slot), k_at(slot), rel_send.at[k + 1, 0], ksem.at[slot], twin),
            send(v_at(slot), v_at(slot), rel_send.at[k + 1, 1], vsem.at[slot], twin),
        )

    def pull_entry(k):
        await_kv(chip(y + out_dir * k) * 2 + c)
        for copy in forwards(k):
            copy.start()

    def pull_mate(k):
        await_kv(chip(mate_chip - out_dir * k) * 2 + c)
        for copy in relays(k):
            copy.start()

    def update(i, key_chip, diagonal):
        keys = kbuf[pl.ds(2 * key_chip, 2)].reshape(2 * rows, HD)
        vals = vbuf[pl.ds(2 * key_chip, 2)].reshape(2 * rows, 2 * HD)
        scores = lax.dot_general(
            qbuf[i], keys, (((1,), (1,)), ((), ())), preferred_element_type=jnp.float32
        )
        if diagonal:
            r = lax.broadcasted_iota(jnp.int32, scores.shape, 0)
            at = jnp.where(r >= half, r - half + rows, r) + c * half
            scores = jnp.where(lax.broadcasted_iota(jnp.int32, scores.shape, 1) <= at, scores, -jnp.inf)
        before = mbuf[i]
        now = jnp.maximum(before, jnp.max(scores, axis=1, keepdims=True))
        mbuf[i] = now
        decay = jnp.exp2((before - now) * factor)
        wide = jnp.concatenate([now] * (2 * rows // HD), axis=1) if 2 * rows > HD else now[:, : 2 * rows]
        weights = jnp.exp2((scores - wide) * factor).astype(jnp.bfloat16)
        acc[i] = acc[i] * jnp.concatenate([decay, decay], axis=1) + jnp.dot(
            weights, vals, preferred_element_type=jnp.float32
        )

    def attend(key_chip):
        def one(i, _):
            query_chip = chip(y + out_dir * i)

            @pl.when(query_chip > key_chip)
            def _():
                update(i, key_chip, False)

            @pl.when(query_chip == key_chip)
            def _():
                update(i, key_chip, True)

            return 0

        lax.fori_loop(0, 4, one, 0)

    pull_mate(0)
    for copy in own:
        copy.wait()
    send(q_slot(0), qbuf.at[0, pl.ds(pl.multiple_of((1 - c) * half, half), half), :], local_sem.at[0],
         qsem.at[0, 1 - c], twin).wait_recv()
    for k in (1, 2, 3):
        for core in range(2):
            send(q_slot(k), qbuf.at[k, pl.ds(core * half, half), :], local_sem.at[0], qsem.at[k, core], twin).wait_recv()

    def stage(k, _):
        @pl.when(k < 4)
        def _():
            pull_entry(k)

        key_chip = chip(y + out_dir * (k - 1))
        await_kv(key_chip * 2 + 1 - c)
        attend(key_chip)

        @pl.when(k < 4)
        def _():
            pull_mate(k)

        key_chip = chip(mate_chip - out_dir * (k - 1))
        await_kv(key_chip * 2 + 1 - c)
        attend(key_chip)
        return 0

    lax.fori_loop(1, 5, stage, 0)

    my_rows = pl.ds(pl.multiple_of(c * half, half), half)

    def finish(i):
        obuf[i] = (acc[i, :, :HD] / acc[i, :, HD:]).astype(jnp.bfloat16)

    back = []
    for i in (3, 2, 1):
        finish(i)
        for core in range(2):
            back.append(
                send(obuf.at[i, pl.ds(core * half, half), :], abuf.at[head, my_rows, :], o_send.at[i, core],
                     asem.at[head, c], chip(y + out_dir * i) * 2 + core)
            )
            back[-1].start()
    finish(0)
    back.append(
        send(obuf.at[0, pl.ds(pl.multiple_of((1 - c) * half, half), half), :], abuf.at[head, my_rows, :],
             o_send.at[0, 0], asem.at[head, c], twin)
    )
    back[-1].start()
    abuf[head, my_rows, :] = obuf[0, my_rows, :]

    kinds = jnp.broadcast_to(mod_ref[...].astype(jnp.float32), (HD, rows)).T
    image = kinds > 0.5
    w_copy.wait()
    for other in range(4):
        for core in range(2):
            @pl.when(jnp.logical_or(head != other, c != core))
            def _():
                send(abuf.at[other, pl.ds(core * half, half), :], abuf.at[other, pl.ds(core * half, half), :],
                     local_sem.at[0], asem.at[other, core], twin).wait_recv()
    for other in range(4):
        piece = abuf[other]
        zero = jnp.zeros_like(piece)
        acat[:, other * HD : (other + 1) * HD] = jnp.where(image, zero, piece)
        acat[:, (other + 4) * HD : (other + 5) * HD] = jnp.where(image, piece, zero)

    def project(step):
        block = lax.rem(z + step + N_TP, N_TP)
        psum[step % N_TP] = jnp.dot(
            acat[...], wbuf[:, pl.ds(pl.multiple_of(block * cols, cols), cols)], preferred_element_type=jnp.float32
        )

    near = (right, left)
    parts = (4, 3, 3, 2, 2, 1, 1)

    def part_rows(way, m):
        low = (m % 2 == 0) == (way == 0)
        return pl.ds(0 if low else half, half)

    def ring_copy(way, m):
        return pltpu.make_async_remote_copy(
            src_ref=rsnd.at[way, m], dst_ref=rrcv.at[way, m], send_sem=r_send.at[way, m], recv_sem=rsem.at[way, m],
            device_id={"tp": near[way]}, device_id_type=MESH,
        )

    def own_part(way, m):
        step = parts[m] if way == 0 else N_TP - parts[m]
        return psum[step % N_TP, part_rows(way, m), :]

    project(4)
    for way in range(2):
        rsnd[way, 0] = own_part(way, 0).astype(jnp.bfloat16)
        ring_copy(way, 0).start()
    for way in range(2):
        project(3 - 6 * way)
        rsnd[way, 1] = own_part(way, 1).astype(jnp.bfloat16)
        ring_copy(way, 1).start()
    for step in (2, -2, 1, -1, 0):
        project(step)
    for m in range(2, 7):
        for way in range(2):
            ring_copy(way, m - 2).wait_recv()
            rsnd[way, m] = (own_part(way, m) + rrcv[way, m - 2].astype(jnp.float32)).astype(jnp.bfloat16)
            ring_copy(way, m).start()
    for way in range(2):
        for m in (5, 6):
            ring_copy(way, m).wait_recv()
    for low, (a, b) in enumerate(((5, 6), (6, 5))):
        span = pl.ds(0 if low else half, half)
        out_ref[span, :] = (
            psum[0, span, :] + rrcv[0, a].astype(jnp.float32) + rrcv[1, b].astype(jnp.float32)
        ).astype(jnp.bfloat16)

    for copy in pending + back:
        copy.wait_send()
    for k in (1, 2, 3):
        for copy in forwards(k):
            copy.wait_send()
    for k in (0, 1, 2, 3):
        for copy in relays(k):
            copy.wait_send()
    for way in range(2):
        for m in range(7):
            ring_copy(way, m).wait_send()


def on_device(queries, key_rows, values, modality, out_weight):
    rows, width = queries.shape
    cols = out_weight.shape[2] // N_TP
    half = rows // 2
    bf, f32 = jnp.bfloat16, jnp.float32
    dma = pltpu.SemaphoreType.DMA
    anywhere = pl.BlockSpec(memory_space=pl.ANY)
    vmem = pl.BlockSpec(memory_space=pltpu.VMEM)
    return pl.pallas_call(
        fused,
        out_shape=jax.ShapeDtypeStruct((rows, cols), bf),
        in_specs=[anywhere, anywhere, anywhere, vmem, anywhere],
        out_specs=vmem,
        scratch_shapes=[
            pltpu.VMEM((4, rows, HD), bf),
            pltpu.VMEM((16, rows, HD), bf),
            pltpu.VMEM((16, rows, 2 * HD), bf),
            pltpu.VMEM((4, rows, HD), f32),
            pltpu.VMEM((4, rows, 2 * HD), f32),
            pltpu.VMEM((4, rows, HD), bf),
            pltpu.VMEM((4, rows, HD), bf),
            pltpu.VMEM((rows, 2 * width), bf),
            pltpu.VMEM((2 * width, out_weight.shape[2]), bf),
            pltpu.VMEM((N_TP, rows, cols), f32),
            pltpu.VMEM((2, 7, half, cols), bf),
            pltpu.VMEM((2, 7, half, cols), bf),
            dma((2,)), dma((16,)), dma((16,)), dma((4, 2)), dma((4, 2)), dma((2, 7)),
            dma((4, 2)), dma((4, 2)), dma((4, 4)), dma((5, 2)), dma((4, 2)), dma((2, 7)),
        ],
        compiler_params=pltpu.CompilerParams(
            collective_id=0, has_side_effects=True, vmem_limit_bytes=56 * 1024 * 1024
        ),
    )(queries, key_rows, values, modality.reshape(1, rows), out_weight.reshape(2 * width, out_weight.shape[2]))


def solution(mesh):
    in_specs = (
        P(("dp", "seq"), "tp"),
        P(("dp", "seq"), "tp"),
        P(("dp", "seq"), "tp"),
        P(("dp", "seq")),
        P(None, "tp", None),
    )
    out_specs = P(("dp", "seq"), "tp")
    return jax.shard_map(
        on_device, mesh=mesh, in_specs=in_specs, out_specs=out_specs, check_vma=False
    )
```

time: 202 us -> 93.1 us (0.46)
  Pallas kernels: 0 us -> 91.3 us
  waiting for transfers between devices: 76.2 us -> 0 us
  blocking collectives: 59.6 us -> 0 us
  starting transfers between devices: 28.2 us -> 0 us
  matrix products: 16.5 us -> 0 us
  local copies, waits for them, and re-layouts: 13 us -> 1.67 us
  other arithmetic: 4.98 us -> 0 us
    pallas_call x0 -> x1, Pallas kernels: none -> 91.3 us  [on_device(): pl.pallas_call(fused, out_shape=jax.ShapeDtypeStruct((rows, cols), bf), i...]
    all_to_all x4 -> x0, waiting for transfers between devices: 76.2 us -> none  [the longest x1 27.9 us: on_device(): lax.all_to_all(spread(values), 'seq', split_axis=0, concat_axis=1, tiled=...]
    all_to_all x1 -> x0, blocking collectives: 59.6 us -> none  [sum_at_owner(): lax.all_to_all(blocks, axis, split_axis=0, concat_axis=0, tiled=True)]
    all_to_all x4 -> x0, starting transfers between devices: 28.2 us -> none  [the longest x1 17.4 us: on_device(): lax.all_to_all(query_items, 'seq', split_axis=0, concat_axis=1, tiled=True)]
    dot_general x6 -> x0, matrix products: 16.5 us -> none  [the longest x2 7 us: single(): jnp.dot(tile_block, out_weight[first_kind], preferred_element_type=jnp.fl...]
    reshape x4 -> x0, local copies, waits for them, and re-layouts: 3.8 us -> none  [the longest x2 2.03 us: spread(): field.reshape(token_rows, head_sets, per_device, head_width)]
    reduce_sum x3 -> x0, other arithmetic: 3.6 us -> none  [the longest x2 2.55 us: one_block(): jnp.sum(weights, axis=2, keepdims=True)]
    broadcast_in_dim x6 -> x0, local copies, waits for them, and re-layouts: 3.48 us -> none  [the longest x4 2.42 us: spread(): jnp.broadcast_to(shaped[:, None], (head_sets, groups, token_rows, per_dev...]
  transfers between devices with their start and end apart: 4 -> 0, of which waited for: 4 -> 0; matrix products, arithmetic and copies ran while one was open for 1% -> 0% of each run, Pallas kernels for 0% -> 0%
where the time goes in v1:
time: 93.1 us; the launch traced here: 93 us
  Pallas kernels  91.3 us (98%)
  local copies, waits for them, and re-layouts  1.67 us (2%)
    pallas_call x1, Pallas kernels, on_device(): pl.pallas_call(fused, out_shape=jax.ShapeDtypeStruct((rows, cols), bf), i...  91.3 us

profile of v1, /device:TPU:1, one launch (start us, length us, event | category | flops | bytes accessed | tf_op | source)
XLA Modules:
  0.0 93.0 jit_solution(15713854994293453870)
XLA Ops:
  0.0 91.3 %shard_map.55 = bf16[256,512]{1,0:T(8,128)(2,1)} custom-call(bf16[256,512]{1,0:T(8,128)(2,1)} %q_hbm.1, bf16[256,512]{1,0:T(8,128)(2,1)} %k_hbm.1, bf16[256,512]{1,0:T(8,128)(2,1)} %v_hbm.1, s32[1,256]{1,0:T(1,128)} %bitcast.3, bf16[1024,4096]{1,0:T(8,128)(2,1)} %bitcast.2), custom_call_target="tpu_custom_call" | custom-call | tf_op jit(solution)/shard_map/pallas_call | solution.py:314
  91.3 1.7 %copy.7 = bf16[256,512]{1,0:T(8,128)(2,1)} copy(bf16[256,512]{1,0:T(8,128)(2,1)} %shard_map.55) | data formatting | bytes 524288

commit v2 on v1

--- a/solution.py
+++ b/solution.py
@@ -1,5 +1,3 @@
-import functools
-
 import jax
 import jax.numpy as jnp
 from jax import lax
@@ -11,11 +9,12 @@
 N_TP = 8
 MESH = pl.DeviceIdType.MESH
 LOG2E = 1.4426950408889634
+CH = 2
 
 
 def fused(
     q_hbm, k_hbm, v_hbm, mod_ref, w_hbm, out_ref,
-    qbuf, kbuf, vbuf, mbuf, acc, obuf, abuf, acat, wbuf, psum, rsnd, rrcv,
+    qbuf, kbuf, vbuf, mbuf, acc, obuf, abuf, image, acat, wbuf, psum, rsnd, rrcv,
     local_sem, ksem, vsem, qsem, asem, rsem, q_send, kv_send, fwd_send, rel_send, o_send, r_send,
 ):
     me = lax.axis_index("seq")
@@ -99,19 +98,21 @@
     pending.append(send(q_rows(1 - c, head), q_slot(0), q_send.at[0, 0], qsem.at[0, c], twin))
     pending.append(send(head_cols(k_hbm, head), k_at(me), rel_send.at[0, 0], ksem.at[me], twin))
     pending.append(send(head_cols(v_hbm, head), v_at(me), rel_send.at[0, 1], vsem.at[me], twin))
-    for k in (3, 2, 1):
+
+    def add_q(k):
         chip_k = targets[k]
         for core in range(2):
             pending.append(
                 send(q_rows(core, chip_k // 2), q_slot(k), q_send.at[k, core], qsem.at[k, c], chip_k * 2 + core)
             )
-    for k in (2, 3, 1):
-        chip_k = targets[k]
-        pending.append(send(head_cols(k_hbm, chip_k // 2), k_at(me), kv_send.at[k, 0], ksem.at[me], chip_k * 2 + c))
-        pending.append(send(head_cols(v_hbm, chip_k // 2), v_at(me), kv_send.at[k, 1], vsem.at[me], chip_k * 2 + c))
-        if k == 2:
-            pending.append(send(head_cols(k_hbm, head), k_at(me), kv_send.at[0, 0], ksem.at[me], mate))
-            pending.append(send(head_cols(v_hbm, head), v_at(me), kv_send.at[0, 1], vsem.at[me], mate))
+
+    def add_kv(k):
+        chip_k = targets[k] if k else mate_chip
+        seq = mate if k == 0 else chip_k * 2 + c
+        pending.append(send(head_cols(k_hbm, chip_k // 2), k_at(me), kv_send.at[k, 0], ksem.at[me], seq))
+        pending.append(send(head_cols(v_hbm, chip_k // 2), v_at(me), kv_send.at[k, 1], vsem.at[me], seq))
+
+    add_kv(1), add_kv(2), add_kv(3), add_kv(0), add_q(1), add_q(2), add_q(3)
     for copy in pending:
         copy.start()
 
@@ -177,118 +178,140 @@
 
         lax.fori_loop(0, 4, one, 0)
 
-    pull_mate(0)
-    for copy in own:
-        copy.wait()
-    send(q_slot(0), qbuf.at[0, pl.ds(pl.multiple_of((1 - c) * half, half), half), :], local_sem.at[0],
-         qsem.at[0, 1 - c], twin).wait_recv()
-    for k in (1, 2, 3):
-        for core in range(2):
-            send(q_slot(k), qbuf.at[k, pl.ds(core * half, half), :], local_sem.at[0], qsem.at[k, core], twin).wait_recv()
-
-    def stage(k, _):
-        @pl.when(k < 4)
-        def _():
-            pull_entry(k)
-
-        key_chip = chip(y + out_dir * (k - 1))
-        await_kv(key_chip * 2 + 1 - c)
-        attend(key_chip)
-
-        @pl.when(k < 4)
-        def _():
-            pull_mate(k)
-
-        key_chip = chip(mate_chip - out_dir * (k - 1))
-        await_kv(key_chip * 2 + 1 - c)
-        attend(key_chip)
-        return 0
-
-    lax.fori_loop(1, 5, stage, 0)
-
-    my_rows = pl.ds(pl.multiple_of(c * half, half), half)
-
-    def finish(i):
-        obuf[i] = (acc[i, :, :HD] / acc[i, :, HD:]).astype(jnp.bfloat16)
-
+    def attend_events(first, last):
+        def one(event, _):
+            key_chip = chip(jnp.where(event < 4, y + out_dir * event, mate_chip - out_dir * (event - 4)))
+            await_kv(key_chip * 2 + 1 - c)
+            attend(key_chip)
+            return 0
+
+        lax.fori_loop(first, last, one, 0)
+
+    def await_q():
+        for copy in own:
+            copy.wait()
+        send(q_slot(0), qbuf.at[0, pl.ds(pl.multiple_of((1 - c) * half, half), half), :], local_sem.at[0],
+             qsem.at[0, 1 - c], twin).wait_recv()
+        for k in (1, 2, 3):
+            for core in range(2):
+                send(q_slot(k), qbuf.at[k, pl.ds(core * half, half), :], local_sem.at[0], qsem.at[k, core],
+                     twin).wait_recv()
+
+    pull_entry(1), pull_entry(2), pull_entry(3), pull_mate(0)
+    await_q()
+    attend_events(0, 2)
+    pull_mate(1)
+    attend_events(2, 5)
+    pull_mate(2)
+    attend_events(5, 6)
+    pull_mate(3)
+    attend_events(6, 8)
+
+    part = half // CH
     back = []
-    for i in (3, 2, 1):
-        finish(i)
-        for core in range(2):
-            back.append(
-                send(obuf.at[i, pl.ds(core * half, half), :], abuf.at[head, my_rows, :], o_send.at[i, core],
-                     asem.at[head, c], chip(y + out_dir * i) * 2 + core)
-            )
-            back[-1].start()
-    finish(0)
-    back.append(
-        send(obuf.at[0, pl.ds(pl.multiple_of((1 - c) * half, half), half), :], abuf.at[head, my_rows, :],
-             o_send.at[0, 0], asem.at[head, c], twin)
-    )
-    back[-1].start()
-    abuf[head, my_rows, :] = obuf[0, my_rows, :]
+
+    def give_back(r):
+        at = pl.ds(pl.multiple_of(c * half + r * part, part), part)
+        for i in (3, 2, 1, 0):
+            for core in range(2):
+                span = pl.ds(core * half + r * part, part)
+                obuf[i, span, :] = (acc[i, span, :HD] / acc[i, span, HD:]).astype(jnp.bfloat16)
+        for i in (3, 2, 1):
+            for core in range(2):
+                back.append(
+                    send(obuf.at[i, pl.ds(core * half + r * part, part), :], abuf.at[head, at, :],
+                         o_send.at[r, i, core], asem.at[r, head, c], chip(y + out_dir * i) * 2 + core)
+                )
+                back[-1].start()
+        back.append(
+            send(obuf.at[0, pl.ds(pl.multiple_of((1 - c) * half + r * part, part), part), :], abuf.at[head, at, :],
+                 o_send.at[r, 0, 0], asem.at[r, head, c], twin)
+        )
+        back[-1].start()
+        abuf[head, at, :] = obuf[0, at, :]
 
     kinds = jnp.broadcast_to(mod_ref[...].astype(jnp.float32), (HD, rows)).T
-    image = kinds > 0.5
+    image[...] = kinds
+    for r in range(CH):
+        give_back(r)
     w_copy.wait()
-    for other in range(4):
-        for core in range(2):
-            @pl.when(jnp.logical_or(head != other, c != core))
-            def _():
-                send(abuf.at[other, pl.ds(core * half, half), :], abuf.at[other, pl.ds(core * half, half), :],
-                     local_sem.at[0], asem.at[other, core], twin).wait_recv()
-    for other in range(4):
-        piece = abuf[other]
-        zero = jnp.zeros_like(piece)
-        acat[:, other * HD : (other + 1) * HD] = jnp.where(image, zero, piece)
-        acat[:, (other + 4) * HD : (other + 5) * HD] = jnp.where(image, piece, zero)
-
-    def project(step):
+
+    def receive(r):
+        for other in range(4):
+            for core in range(2):
+                @pl.when(jnp.logical_or(head != other, c != core))
+                def _():
+                    landed = abuf.at[other, pl.ds(core * half + r * part, part), :]
+                    send(landed, landed, local_sem.at[0], asem.at[r, other, core], twin).wait_recv()
+        for other in range(4):
+            for core in range(2):
+                span = pl.ds(core * half + r * part, part)
+                piece = abuf[other, span, :]
+                zero = jnp.zeros_like(piece)
+                chosen = image[span, :] > 0.5
+                to = pl.ds(core * part, part)
+                acat[r, to, other * HD : (other + 1) * HD] = jnp.where(chosen, zero, piece)
+                acat[r, to, (other + 4) * HD : (other + 5) * HD] = jnp.where(chosen, piece, zero)
+
+    def project(r, step):
         block = lax.rem(z + step + N_TP, N_TP)
-        psum[step % N_TP] = jnp.dot(
-            acat[...], wbuf[:, pl.ds(pl.multiple_of(block * cols, cols), cols)], preferred_element_type=jnp.float32
+        psum[r, step % N_TP] = jnp.dot(
+            acat[r], wbuf[:, pl.ds(pl.multiple_of(block * cols, cols), cols)], preferred_element_type=jnp.float32
         )
 
     near = (right, left)
     parts = (4, 3, 3, 2, 2, 1, 1)
 
-    def part_rows(way, m):
+    def ring_copy(r, way, m):
+        return pltpu.make_async_remote_copy(
+            src_ref=rsnd.at[r, way, m], dst_ref=rrcv.at[r, way, m], send_sem=r_send.at[r, way, m],
+            recv_sem=rsem.at[r, way, m], device_id={"tp": near[way]}, device_id_type=MESH,
+        )
+
+    def own_part(r, way, m):
+        step = parts[m] if way == 0 else N_TP - parts[m]
         low = (m % 2 == 0) == (way == 0)
-        return pl.ds(0 if low else half, half)
-
-    def ring_copy(way, m):
-        return pltpu.make_async_remote_copy(
-            src_ref=rsnd.at[way, m], dst_ref=rrcv.at[way, m], send_sem=r_send.at[way, m], recv_sem=rsem.at[way, m],
-            device_id={"tp": near[way]}, device_id_type=MESH,
-        )
-
-    def own_part(way, m):
-        step = parts[m] if way == 0 else N_TP - parts[m]
-        return psum[step % N_TP, part_rows(way, m), :]
-
-    project(4)
-    for way in range(2):
-        rsnd[way, 0] = own_part(way, 0).astype(jnp.bfloat16)
-        ring_copy(way, 0).start()
-    for way in range(2):
-        project(3 - 6 * way)
-        rsnd[way, 1] = own_part(way, 1).astype(jnp.bfloat16)
-        ring_copy(way, 1).start()
-    for step in (2, -2, 1, -1, 0):
-        project(step)
-    for m in range(2, 7):
-        for way in range(2):
-            ring_copy(way, m - 2).wait_recv()
-            rsnd[way, m] = (own_part(way, m) + rrcv[way, m - 2].astype(jnp.float32)).astype(jnp.bfloat16)
-            ring_copy(way, m).start()
-    for way in range(2):
-        for m in (5, 6):
-            ring_copy(way, m).wait_recv()
-    for low, (a, b) in enumerate(((5, 6), (6, 5))):
-        span = pl.ds(0 if low else half, half)
-        out_ref[span, :] = (
-            psum[0, span, :] + rrcv[0, a].astype(jnp.float32) + rrcv[1, b].astype(jnp.float32)
-        ).astype(jnp.bfloat16)
+        return psum[r, step % N_TP, pl.ds(0 if low else part, part), :]
+
+    def ring_open(r):
+        receive(r)
+        project(r, 4)
+        for way in range(2):
+            rsnd[r, way, 0] = own_part(r, way, 0).astype(jnp.bfloat16)
+            ring_copy(r, way, 0).start()
+        for way in range(2):
+            project(r, 3 - 6 * way)
+            rsnd[r, way, 1] = own_part(r, way, 1).astype(jnp.bfloat16)
+            ring_copy(r, way, 1).start()
+        for step in (2, -2, 1, -1, 0):
+            project(r, step)
+
+    def ring_step(r, m):
+        for way in range(2):
+            ring_copy(r, way, m - 2).wait_recv()
+            rsnd[r, way, m] = (own_part(r, way, m) + rrcv[r, way, m - 2].astype(jnp.float32)).astype(jnp.bfloat16)
+            ring_copy(r, way, m).start()
+
+    def ring_close(r):
+        for way in range(2):
+            for m in (5, 6):
+                ring_copy(r, way, m).wait_recv()
+        for core, (a, b) in enumerate(((6, 5), (5, 6))):
+            out_ref[pl.ds(core * half + r * part, part), :] = (
+                psum[r, 0, pl.ds(core * part, part), :]
+                + rrcv[r, 0, a].astype(jnp.float32)
+                + rrcv[r, 1, b].astype(jnp.float32)
+            ).astype(out_ref.dtype)
+
+    for slot in range(CH + 6):
+        for r in reversed(range(CH)):
+            phase = slot - r
+            if phase == 0:
+                ring_open(r)
+            elif 1 <= phase <= 5:
+                ring_step(r, phase + 1)
+            elif phase == 6:
+                ring_close(r)
 
     for copy in pending + back:
         copy.wait_send()
@@ -298,9 +321,10 @@
     for k in (0, 1, 2, 3):
         for copy in relays(k):
             copy.wait_send()
-    for way in range(2):
-        for m in range(7):
-            ring_copy(way, m).wait_send()
+    for r in range(CH):
+        for way in range(2):
+            for m in range(7):
+                ring_copy(r, way, m).wait_send()
 
 
 def on_device(queries, key_rows, values, modality, out_weight):
@@ -313,7 +337,7 @@
     vmem = pl.BlockSpec(memory_space=pltpu.VMEM)
     return pl.pallas_call(
         fused,
-        out_shape=jax.ShapeDtypeStruct((rows, cols), bf),
+        out_shape=jax.ShapeDtypeStruct((rows, cols), f32),
         in_specs=[anywhere, anywhere, anywhere, vmem, anywhere],
         out_specs=vmem,
         scratch_shapes=[
@@ -324,18 +348,19 @@
             pltpu.VMEM((4, rows, 2 * HD), f32),
             pltpu.VMEM((4, rows, HD), bf),
             pltpu.VMEM((4, rows, HD), bf),
-            pltpu.VMEM((rows, 2 * width), bf),
+            pltpu.VMEM((rows, HD), f32),
+            pltpu.VMEM((CH, rows // CH, 2 * width), bf),
             pltpu.VMEM((2 * width, out_weight.shape[2]), bf),
-            pltpu.VMEM((N_TP, rows, cols), f32),
-            pltpu.VMEM((2, 7, half, cols), bf),
-            pltpu.VMEM((2, 7, half, cols), bf),
-            dma((2,)), dma((16,)), dma((16,)), dma((4, 2)), dma((4, 2)), dma((2, 7)),
-            dma((4, 2)), dma((4, 2)), dma((4, 4)), dma((5, 2)), dma((4, 2)), dma((2, 7)),
+            pltpu.VMEM((CH, N_TP, rows // CH, cols), f32),
+            pltpu.VMEM((CH, 2, 7, half // CH, cols), bf),
+            pltpu.VMEM((CH, 2, 7, half // CH, cols), bf),
+            dma((2,)), dma((16,)), dma((16,)), dma((4, 2)), dma((CH, 4, 2)), dma((CH, 2, 7)),
+            dma((4, 2)), dma((4, 2)), dma((4, 4)), dma((5, 2)), dma((CH, 4, 2)), dma((CH, 2, 7)),
         ],
         compiler_params=pltpu.CompilerParams(
             collective_id=0, has_side_effects=True, vmem_limit_bytes=56 * 1024 * 1024
         ),
-    )(queries, key_rows, values, modality.reshape(1, rows), out_weight.reshape(2 * width, out_weight.shape[2]))
+    )(queries, key_rows, values, modality.reshape(1, rows), out_weight.reshape(2 * width, out_weight.shape[2])).astype(bf)
 
 
 def solution(mesh):

time: 93.1 us -> 85.8 us (0.922)
  Pallas kernels: 91.3 us -> 83.8 us
  other arithmetic: 0 us -> 1.78 us
  local copies, waits for them, and re-layouts: 1.67 us -> 0 us
    pallas_call x1, Pallas kernels: 91.3 us -> 83.8 us  [on_device(): pl.pallas_call(fused, out_shape=jax.ShapeDtypeStruct((rows, cols), f32),...]
    convert_element_type x0 -> x1, other arithmetic: none -> 1.78 us  [on_device(): return pl.pallas_call(fused, out_shape=jax.ShapeDtypeStruct((rows, cols),...]
    unnamed x1 -> x0, local copies, waits for them, and re-layouts: 1.67 us -> none
where the time goes in v2:
time: 85.8 us; the launch traced here: 85.6 us
  Pallas kernels  83.8 us (98%)
  other arithmetic  1.78 us (2%)
    pallas_call x1, Pallas kernels, on_device(): pl.pallas_call(fused, out_shape=jax.ShapeDtypeStruct((rows, cols), f32),...  83.8 us
    convert_element_type x1, other arithmetic, on_device(): return pl.pallas_call(fused, out_shape=jax.ShapeDtypeStruct((rows, cols),...  1.78 us

profile of v2, /device:TPU:1, one launch (start us, length us, event | category | flops | bytes accessed | tf_op | source)
XLA Modules:
  0.0 85.6 jit_solution(15487688871871957566)
XLA Ops:
  0.0 83.8 %shard_map.55 = f32[256,512]{1,0:T(8,128)} custom-call(bf16[256,512]{1,0:T(8,128)(2,1)} %q_hbm.1, bf16[256,512]{1,0:T(8,128)(2,1)} %k_hbm.1, bf16[256,512]{1,0:T(8,128)(2,1)} %v_hbm.1, s32[1,256]{1,0:T(1,128)} %bitcast.3, bf16[1024,4096]{1,0:T(8,128)(2,1)} %bitcast.2), custom_call_target="tpu_custom_call" | custom-call | tf_op jit(solution)/shard_map/pallas_call | solution.py:338
  83.8 1.8 %convert_element_type.3 = bf16[256,512]{1,0:T(8,128)(2,1)} convert(f32[256,512]{1,0:T(8,128)} %shard_map.55) | non-fusion elementwise | flops 131072 | bytes 786432 | tf_op jit(solution)/shard_map/convert_element_type | solution.py:363

commit v3 on v2

--- a/solution.py
+++ b/solution.py
@@ -10,11 +10,15 @@
 MESH = pl.DeviceIdType.MESH
 LOG2E = 1.4426950408889634
 CH = 2
+PLAN = (
+    ("E", 1), ("E", 2), ("Q",), ("A", 0, 1), ("E", 3), ("M", 0), ("A", 1, 3), ("M", 1), ("A", 3, 5), ("M", 2), ("A", 5, 6),
+    ("M", 3), ("A", 6, 8),
+)
 
 
 def fused(
     q_hbm, k_hbm, v_hbm, mod_ref, w_hbm, out_ref,
-    qbuf, kbuf, vbuf, mbuf, acc, obuf, abuf, image, acat, wbuf, psum, rsnd, rrcv,
+    qbuf, kbuf, vbuf, mbuf, lbuf, vt, acc, obuf, abuf, image, acat, wbuf, psum, rsnd, rrcv,
     local_sem, ksem, vsem, qsem, asem, rsem, q_send, kv_send, fwd_send, rel_send, o_send, r_send,
 ):
     me = lax.axis_index("seq")
@@ -46,7 +50,7 @@
         return kbuf.at[slot]
 
     def v_at(slot):
-        return vbuf.at[slot, :, pl.ds(0, HD)]
+        return vbuf.at[slot]
 
     def head_cols(ref, h):
         return ref.at[:, pl.ds(pl.multiple_of(h * HD, HD), HD)]
@@ -83,7 +87,7 @@
         pl.semaphore_signal(barrier, inc=1, device_id={"tp": neighbour}, device_id_type=MESH)
     mbuf[...] = jnp.full(mbuf.shape, -jnp.inf, jnp.float32)
     acc[...] = jnp.zeros(acc.shape, jnp.float32)
-    vbuf[:, :, HD:] = jnp.ones((vbuf.shape[0], rows, HD), jnp.bfloat16)
+    lbuf[...] = jnp.zeros(lbuf.shape, jnp.float32)
     pl.semaphore_wait(barrier, peers + 3)
 
     targets = {1: chip(y + out_dir), 3: chip(y + 3 * out_dir), 2: chip(y - 2 * out_dir)}
@@ -112,7 +116,7 @@
         pending.append(send(head_cols(k_hbm, chip_k // 2), k_at(me), kv_send.at[k, 0], ksem.at[me], seq))
         pending.append(send(head_cols(v_hbm, chip_k // 2), v_at(me), kv_send.at[k, 1], vsem.at[me], seq))
 
-    add_kv(1), add_kv(2), add_kv(3), add_kv(0), add_q(1), add_q(2), add_q(3)
+    add_kv(1), add_kv(2), add_q(1), add_q(3), add_q(2), add_kv(3), add_kv(0)
     for copy in pending:
         copy.start()
 
@@ -142,41 +146,64 @@
         for copy in relays(k):
             copy.start()
 
-    def update(i, key_chip, diagonal):
+    def update(blocks, key_chip, diagonal):
         keys = kbuf[pl.ds(2 * key_chip, 2)].reshape(2 * rows, HD)
-        vals = vbuf[pl.ds(2 * key_chip, 2)].reshape(2 * rows, 2 * HD)
-        scores = lax.dot_general(
-            qbuf[i], keys, (((1,), (1,)), ((), ())), preferred_element_type=jnp.float32
-        )
+        scores = [
+            lax.dot_general(keys, qbuf[i], (((1,), (1,)), ((), ())), preferred_element_type=jnp.float32)
+            for i in blocks
+        ]
         if diagonal:
-            r = lax.broadcasted_iota(jnp.int32, scores.shape, 0)
-            at = jnp.where(r >= half, r - half + rows, r) + c * half
-            scores = jnp.where(lax.broadcasted_iota(jnp.int32, scores.shape, 1) <= at, scores, -jnp.inf)
-        before = mbuf[i]
-        now = jnp.maximum(before, jnp.max(scores, axis=1, keepdims=True))
-        mbuf[i] = now
-        decay = jnp.exp2((before - now) * factor)
-        wide = jnp.concatenate([now] * (2 * rows // HD), axis=1) if 2 * rows > HD else now[:, : 2 * rows]
-        weights = jnp.exp2((scores - wide) * factor).astype(jnp.bfloat16)
-        acc[i] = acc[i] * jnp.concatenate([decay, decay], axis=1) + jnp.dot(
-            weights, vals, preferred_element_type=jnp.float32
-        )
+            q = lax.broadcasted_iota(jnp.int32, scores[0].shape, 1)
+            at = jnp.where(q >= half, q - half + rows, q) + c * half
+            seen = lax.broadcasted_iota(jnp.int32, scores[0].shape, 0) <= at
+            scores = [jnp.where(seen, s, -jnp.inf) for s in scores]
+        state = [(mbuf[i], lbuf[i], acc[i]) for i in blocks]
+        fresh = []
+        for s, (top, total, sums) in zip(scores, state):
+            now = jnp.maximum(top, jnp.max(s, axis=0, keepdims=True))
+            decay = jnp.exp2((top - now) * factor)
+            weights = jnp.exp2((s - now) * factor)
+            total = total * decay + jnp.sum(weights, axis=0, keepdims=True)
+            sums = sums * decay + jnp.dot(
+                vt[...], weights.astype(jnp.bfloat16), preferred_element_type=jnp.float32
+            )
+            fresh.append((now, total, sums))
+        for i, (now, total, sums) in zip(blocks, fresh):
+            mbuf[i], lbuf[i], acc[i] = now, total, sums
 
     def attend(key_chip):
-        def one(i, _):
+        vt[...] = vbuf[pl.ds(2 * key_chip, 2)].reshape(2 * rows, HD).T
+
+        def one(i):
             query_chip = chip(y + out_dir * i)
 
             @pl.when(query_chip > key_chip)
             def _():
-                update(i, key_chip, False)
+                update((i,), key_chip, False)
 
             @pl.when(query_chip == key_chip)
             def _():
-                update(i, key_chip, True)
+                update((i,), key_chip, True)
+
+        def pair(j, _):
+            first, second = 2 * j + 1, lax.rem(2 * j + 2, 4)
+            lower = jnp.minimum(chip(y + out_dir * first), chip(y + out_dir * second))
+
+            @pl.when(lower > key_chip)
+            def _():
+                update((first, second), key_chip, False)
+
+            @pl.when(lower <= key_chip)
+            def _():
+                def each(t, _):
+                    one(jnp.where(t == 0, first, second))
+                    return 0
+
+                lax.fori_loop(0, 2, each, 0)
 
             return 0
 
-        lax.fori_loop(0, 4, one, 0)
+        lax.fori_loop(0, 2, pair, 0)
 
     def attend_events(first, last):
         def one(event, _):
@@ -197,25 +224,14 @@
                 send(q_slot(k), qbuf.at[k, pl.ds(core * half, half), :], local_sem.at[0], qsem.at[k, core],
                      twin).wait_recv()
 
-    pull_entry(1), pull_entry(2), pull_entry(3), pull_mate(0)
-    await_q()
-    attend_events(0, 2)
-    pull_mate(1)
-    attend_events(2, 5)
-    pull_mate(2)
-    attend_events(5, 6)
-    pull_mate(3)
-    attend_events(6, 8)
+    for kind, *span in PLAN:
+        {"E": pull_entry, "M": pull_mate, "Q": await_q, "A": attend_events}[kind](*span)
 
     part = half // CH
     back = []
 
     def give_back(r):
         at = pl.ds(pl.multiple_of(c * half + r * part, part), part)
-        for i in (3, 2, 1, 0):
-            for core in range(2):
-                span = pl.ds(core * half + r * part, part)
-                obuf[i, span, :] = (acc[i, span, :HD] / acc[i, span, HD:]).astype(jnp.bfloat16)
         for i in (3, 2, 1):
             for core in range(2):
                 back.append(
@@ -232,6 +248,8 @@
 
     kinds = jnp.broadcast_to(mod_ref[...].astype(jnp.float32), (HD, rows)).T
     image[...] = kinds
+    for i in range(4):
+        obuf[i] = (acc[i] / lbuf[i]).T.astype(jnp.bfloat16)
     for r in range(CH):
         give_back(r)
     w_copy.wait()
@@ -283,14 +301,14 @@
             project(r, 3 - 6 * way)
             rsnd[r, way, 1] = own_part(r, way, 1).astype(jnp.bfloat16)
             ring_copy(r, way, 1).start()
-        for step in (2, -2, 1, -1, 0):
-            project(r, step)
 
     def ring_step(r, m):
         for way in range(2):
             ring_copy(r, way, m - 2).wait_recv()
             rsnd[r, way, m] = (own_part(r, way, m) + rrcv[r, way, m - 2].astype(jnp.float32)).astype(jnp.bfloat16)
             ring_copy(r, way, m).start()
+        for step in {2: (2, -2), 4: (1, -1), 6: (0,)}.get(m, ()):
+            project(r, step)
 
     def ring_close(r):
         for way in range(2):
@@ -343,9 +361,11 @@
         scratch_shapes=[
             pltpu.VMEM((4, rows, HD), bf),
             pltpu.VMEM((16, rows, HD), bf),
-            pltpu.VMEM((16, rows, 2 * HD), bf),
-            pltpu.VMEM((4, rows, HD), f32),
-            pltpu.VMEM((4, rows, 2 * HD), f32),
+            pltpu.VMEM((16, rows, HD), bf),
+            pltpu.VMEM((4, 1, rows), f32),
+            pltpu.VMEM((4, 1, rows), f32),
+            pltpu.VMEM((HD, 2 * rows), bf),
+            pltpu.VMEM((4, HD, rows), f32),
             pltpu.VMEM((4, rows, HD), bf),
             pltpu.VMEM((4, rows, HD), bf),
             pltpu.VMEM((rows, HD), f32),

time: 85.8 us -> 83.4 us (0.972)
  Pallas kernels: 83.8 us -> 81.4 us
    pallas_call x1, Pallas kernels: 83.8 us -> 81.4 us  [on_device(): pl.pallas_call(fused, out_shape=jax.ShapeDtypeStruct((rows, cols), f32),...]
where the time goes in v3:
time: 83.4 us; the launch traced here: 83.2 us
  Pallas kernels  81.4 us (98%)
  other arithmetic  1.78 us (2%)
    pallas_call x1, Pallas kernels, on_device(): pl.pallas_call(fused, out_shape=jax.ShapeDtypeStruct((rows, cols), f32),...  81.4 us
    convert_element_type x1, other arithmetic, on_device(): return pl.pallas_call(fused, out_shape=jax.ShapeDtypeStruct((rows, cols),...  1.78 us

profile of v3, /device:TPU:1, one launch (start us, length us, event | category | flops | bytes accessed | tf_op | source)
XLA Modules:
  0.0 83.2 jit_solution(7149880325683654995)
XLA Ops:
  0.0 81.4 %shard_map.55 = f32[256,512]{1,0:T(8,128)} custom-call(bf16[256,512]{1,0:T(8,128)(2,1)} %q_hbm.1, bf16[256,512]{1,0:T(8,128)(2,1)} %k_hbm.1, bf16[256,512]{1,0:T(8,128)(2,1)} %v_hbm.1, s32[1,256]{1,0:T(1,128)} %bitcast.3, bf16[1024,4096]{1,0:T(8,128)(2,1)} %bitcast.2), custom_call_target="tpu_custom_call" | custom-call | tf_op jit(solution)/shard_map/pallas_call | solution.py:356
  81.4 1.8 %convert_element_type.3 = bf16[256,512]{1,0:T(8,128)(2,1)} convert(f32[256,512]{1,0:T(8,128)} %shard_map.55) | non-fusion elementwise | flops 131072 | bytes 786432 | tf_op jit(solution)/shard_map/convert_element_type | solution.py:383
